TPU v7x, 768 devices: a whole 4x8x12 slice. The times are simulated.
768 devices in a mesh: blk: 128 (over y, z_hi, x), grp: 6 (over z_lo, core).
Axes of the slice: x: 4, y: 8, z: 12 (z_hi: 4, z_lo: 3; z = z_hi * 3 + z_lo), core: 2. Of those that a mesh axis runs over, the one named last changes fastest.
Arguments:
- text: bfloat16 [128, 1152, 1024], P('blk', 'grp'), may hold values from -64 to 64
- image: bfloat16 [128, 1152, 1024], P('blk', 'grp'), may hold values from -64 to 64
- pair_index: int32 [128, 1152], P('blk', 'grp'), may hold values from 0 to 1151, each once within a row
Outputs:
- grad_text: float32 [128, 1152, 1024], P('blk', 'grp')
- grad_image: float32 [128, 1152, 1024], P('blk', 'grp')
- loss: float32 [], replicated
Inputs may be any that keep to these rules, and one draw needn't show every extreme that they name: Every sub-batch's row of pair_index names each of 0 to 1151 once.
All inputs are finite; a program needn't handle non-finite values.
Results may differ from a plain program's by a relative error of at most 0.0024.
Values may be sent and summed in bfloat16 or wider, within the bound.
A program may use at most 32 MiB of HBM per device.

v0:
```python
import jax
import jax.numpy as jnp
from jax import lax
from jax.sharding import Mesh
from jax.sharding import PartitionSpec as P

GRP = ("grp_0", "grp_1")
BLK_GRP = ("blk_0", "blk_1", "blk_2", "grp_0", "grp_1")
BLK = ("blk_0", "blk_1", "blk_2")


score_scale = 0.125


def joined_along(parts, dim):
    parts = jnp.moveaxis(parts, 0, dim)
    dims = parts.shape
    return parts.reshape(*dims[:dim], dims[dim] * dims[dim + 1], *dims[dim + 2 :])


def sent_to_all(x, axis):
    copies = jnp.broadcast_to(x, (lax.axis_size(axis), *x.shape))
    return lax.all_to_all(copies, axis, split_axis=0, concat_axis=0, tiled=True)


def collect(x, axis, dim):
    return joined_along(sent_to_all(x, axis), dim)


def collected_together(x, axis):
    leaves = jax.tree.leaves(x)
    order = sorted(range(len(leaves)), key=lambda k: -leaves[k].size)
    width = (1, *leaves[order[0]].shape)[-1]
    lines = [
        jnp.pad(leaves[k].reshape(-1), (0, -leaves[k].size % width)).reshape(-1, width)
        for k in order
    ]
    both, at, found = (lax.all_gather(jnp.concatenate(lines), axis), 0, {})
    for k, line in zip(order, lines):
        piece = both[:, at : at + len(line)].reshape(len(both), -1)
        found[k] = piece[:, : leaves[k].size].reshape(-1, *leaves[k].shape)
        at += len(line)
    numbers = iter(range(len(leaves)))
    return jax.tree.map(lambda _: found[next(numbers)], x)


def combined_all(x, axis, combine):
    everything = collected_together(x, axis)
    initial = jax.tree.map(lambda part: part[0], everything)

    def hop(k, so_far):
        return combine(so_far, jax.tree.map(lambda part: part[k], everything))

    return lax.fori_loop(1, lax.axis_size(axis), hop, initial)


def gather_turned(arrays, axis, dims):
    turned = [jnp.moveaxis(a, dim, 0) for a, dim in zip(arrays, dims)]
    both = jnp.concatenate([t.reshape(len(t), -1) for t in turned], axis=1)
    out, at, done = (lax.all_gather(both, axis, axis=0, tiled=True), 0, [])
    for t, dim in zip(turned, dims):
        piece = out[:, at : at + t[0].size].reshape(-1, *t.shape[1:])
        done.append(jnp.moveaxis(piece, 0, dim))
        at += t[0].size
    return tuple(done)


def by_axis(x, axes):
    for axis in axes:
        x = lax.psum(x, axis)
    return x


def join_stats(left, right):
    top = jnp.maximum(left[0], right[0])
    return (top, left[1] * jnp.exp(left[0] - top) + right[1] * jnp.exp(right[0] - top))


def local(text, image, pair_index):
    local_text = text[0]
    own_image = image[0]
    pairs = pair_index[0]
    rows = local_text.shape[0]
    width = local_text.shape[1]
    total = rows * lax.axis_size(GRP)
    offset = lax.axis_index(GRP) * rows

    def scores_of(block):
        return (
            jnp.einsum("rd,nd->rn", local_text, block, preferred_element_type=jnp.float32)
            * score_scale
        )

    def hits_of(count):
        ids = jnp.arange(count, dtype=jnp.int32)
        return pairs[:, None] == ids[None, :]

    start_carry = (
        jnp.full((rows,), -1e30, jnp.float32),
        jnp.zeros((rows,), jnp.float32),
        jnp.zeros((total,), jnp.float32),
        jnp.zeros((total,), jnp.float32),
        jnp.zeros((rows,), jnp.float32),
    )
    start_carry = start_carry + (jnp.zeros((total, width), jnp.bfloat16),)
    block = collect(image, GRP, 1)[0]
    count = block.shape[0]
    scores = scores_of(block)
    row_top = jnp.maximum(start_carry[0], jnp.max(scores, axis=1))
    row_total = jnp.sum(jnp.exp(scores - row_top[:, None]), axis=1)
    col_top = jnp.max(scores, axis=0)
    col_total = jnp.sum(jnp.exp(scores - col_top[None, :]), axis=0)
    col_tops = col_top
    col_totals = col_total
    positive = jnp.sum(jnp.where(hits_of(count), scores, 0.0), axis=1)
    result = (row_top, row_total, col_tops, col_totals, positive)
    result = result + (block,)
    carried = result
    row_lse = carried[0] + jnp.log(carried[1])
    positive = carried[4]
    col_top, col_total = combined_all((carried[2], carried[3]), GRP, join_stats)
    col_lse = col_top + jnp.log(col_total)
    block = carried[5][None][0]
    count = block.shape[0]
    scores = scores_of(block)
    weight = (
        jnp.exp(scores - row_lse[:, None])
        + jnp.exp(scores - col_lse[None, :])
        - 2.0 * hits_of(count).astype(jnp.float32)
    ).astype(jnp.bfloat16)
    result = (jnp.dot(weight, block, preferred_element_type=jnp.float32),)
    grad_text = result[0] * (score_scale * 0.5)
    all_lse, pair_values = gather_turned((row_lse, pairs.astype(jnp.float32)), GRP, (0, 0))
    all_pairs = pair_values.astype(jnp.int32)
    own_ids = offset + jnp.arange(rows, dtype=jnp.int32)
    own_col = lax.dynamic_slice_in_dim(col_lse, offset, rows, 0)
    piece = lax.all_gather(local_text, GRP, axis=0, tiled=True)
    count = piece.shape[0]
    flipped = (
        jnp.einsum("nd,kd->nk", own_image, piece, preferred_element_type=jnp.float32) * score_scale
    )
    hit_back = (all_pairs[None, :] == own_ids[:, None]).astype(jnp.float32)
    weight_back = (
        jnp.exp(flipped - all_lse[None, :]) + jnp.exp(flipped - own_col[:, None]) - 2.0 * hit_back
    ).astype(jnp.bfloat16)
    summed = jnp.dot(weight_back, piece, preferred_element_type=jnp.float32)
    grad_image = summed * (score_scale * 0.5)
    own_lse = lax.dynamic_slice_in_dim(col_lse, offset, rows, 0)
    partial_sum = jnp.sum(row_lse - 2.0 * positive) + jnp.sum(own_lse)
    loss = by_axis(partial_sum, BLK_GRP) / (2.0 * total * lax.axis_size(BLK))
    return (grad_text[None], grad_image[None], loss)


def solution(mesh):
    torus = Mesh(mesh.devices.reshape(8, 4, 4, 3, 2), ("blk_0", "blk_1", "blk_2", "grp_0", "grp_1"))
    in_specs = (P(BLK, GRP, None), P(BLK, GRP, None), P(BLK, GRP))
    out_specs = (P(BLK, GRP, None), P(BLK, GRP, None), P())
    return jax.shard_map(local, mesh=torus, in_specs=in_specs, out_specs=out_specs, check_vma=False)
```

profile of v0, /device:TPU:1, one launch (start us, length us, event | category | flops | bytes accessed | tf_op | source)
XLA Modules:
  0.0 167.0 jit_solution(14419092173719719087)
XLA Ops:
  7.2 2.7 %broadcast_in_dim.10 = bf16[6,1,192,1024]{3,2,1,0:T(8,128)(2,1)} broadcast(bf16[192,1024]{1,0:T(8,128)(2,1)} %bitcast.45), dimensions={2,3} | broadcast | bytes 2752512 | tf_op jit(solution)/shard_map/broadcast_in_dim | solution.py:22
  9.9 14.0 %all-to-all-start = ((bf16[6,1,192,1024]{3,2,1,0:T(8,128)(2,1)}), bf16[6,1,192,1024]{3,2,1,0:T(8,128)(2,1)S(1)}, u32[]{:S(2)}, u32[]{:S(2)}) async-start(bf16[6,1,192,1024]{3,2,1,0:T(8,128)(2,1)} %broadcast_in_dim.10), calls=%async_computation | async-start | bytes 4718592 | tf_op jit(solution)/shard_map/all_to_all | solution.py:23
  23.9 0.0 copy-start
  23.9 0.0 all-gather.6.cloned.1.call-start
  23.9 0.7 all-gather.6.cloned.1.call-update
  24.6 49.2 %all-to-all-done = bf16[6,1,192,1024]{3,2,1,0:T(8,128)(2,1)S(1)} async-done(((bf16[6,1,192,1024]{3,2,1,0:T(8,128)(2,1)}), bf16[6,1,192,1024]{3,2,1,0:T(8,128)(2,1)S(1)}, u32[]{:S(2)}, u32[]{:S(2)}) %all-to-all-start) | async-done | bytes 2359328 | tf_op jit(solution)/shard_map/all_to_all | solution.py:23
  73.8 2.0 %fusion.36 = (f32[192]{0:T(256)S(1)}, f32[1152]{0:T(1024)S(1)}, f32[192,1152]{1,0:T(8,128)S(1)}) fusion(bf16[1152,1024]{1,0:T(8,128)(2,1)S(1)} %bitcast.43, bf16[1,192,1024]{2,1,0:T(8,128)(2,1)} %param.5), kind=kOutput, calls=%fused_computation.53 | convolution fusion | flops 453647040 | bytes 3642624 | tf_op jit(solution)/shard_map/rd,nd->rn/dot_general | solution.py:90
  75.9 0.0 copy-done
  75.9 0.5 select_reduce_fusion
  76.4 10.1 %all-gather.2 = f32[6,2,1152]{2,1,0:T(2,128)S(1)} all-gather(f32[1,2,1152]{2,1,0:T(2,128)S(1)} %maximum_bitcast_fusion), channel_id=2, replica_groups=mesh['blk_0'=8,'blk_1'=4,'blk_2'=4,'grp_0'=3,'grp_1'=2] {'grp_0','grp_1'}, dimensions={0}, use_global_device_ids=true | all-gather | bytes 64512 | tf_op jit(solution)/shard_map/all_gather | solution.py:38
  86.6 0.4 while.17
  87.0 0.7 fusion.37
  87.7 0.6 subtract_reduce_fusion
  89.6 11.2 %psum.35 = f32[]{:T(128)} all-reduce(f32[]{:T(128)S(6)} %add.106), channel_id=1, replica_groups=mesh['blk_0'=8,'blk_1'=4,'blk_2'=4,'grp_0'=3,'grp_1'=2] {'blk_0'}, use_global_device_ids=true, to_apply=%region_9.10 | all-reduce | flops 1 | bytes 8 | tf_op jit(solution)/shard_map/psum | solution.py:70
  100.8 15.2 %psum.36 = f32[]{:T(128)} all-reduce(f32[]{:T(128)} %psum.35), channel_id=1, replica_groups=mesh['blk_0'=8,'blk_1'=4,'blk_2'=4,'grp_0'=3,'grp_1'=2] {'blk_1'}, use_global_device_ids=true, to_apply=%region_10.11 | all-reduce | flops 1 | bytes 8 | tf_op jit(solution)/shard_map/psum | solution.py:70
  116.0 9.1 %psum.37 = f32[]{:T(128)} all-reduce(f32[]{:T(128)} %psum.36), channel_id=1, replica_groups=mesh['blk_0'=8,'blk_1'=4,'blk_2'=4,'grp_0'=3,'grp_1'=2] {'blk_2'}, use_global_device_ids=true, to_apply=%region_11.12 | all-reduce | flops 1 | bytes 8 | tf_op jit(solution)/shard_map/psum | solution.py:70
  125.1 5.3 %psum.38 = f32[]{:T(128)} all-reduce(f32[]{:T(128)} %psum.37), channel_id=1, replica_groups=mesh['blk_0'=8,'blk_1'=4,'blk_2'=4,'grp_0'=3,'grp_1'=2] {'grp_0'}, use_global_device_ids=true, to_apply=%region_12.13 | all-reduce | flops 1 | bytes 8 | tf_op jit(solution)/shard_map/psum | solution.py:70
  130.4 11.8 %psum.39 = f32[]{:T(128)} all-reduce(f32[]{:T(128)} %psum.38), channel_id=1, replica_groups=mesh['blk_0'=8,'blk_1'=4,'blk_2'=4,'grp_0'=3,'grp_1'=2] {'grp_1'}, use_global_device_ids=true, to_apply=%region_13.14 | all-reduce | flops 1 | bytes 8 | tf_op jit(solution)/shard_map/psum | solution.py:70
  142.3 9.3 %all-gather.3 = f32[6,192,2]{1,2,0:T(2,128)S(1)} all-gather(f32[1,192,2]{1,2,0:T(2,128)S(1)} %maximum_bitcast_fusion.1), channel_id=1, replica_groups=mesh['blk_0'=8,'blk_1'=4,'blk_2'=4,'grp_0'=3,'grp_1'=2] {'grp_0','grp_1'}, dimensions={0}, use_global_device_ids=true | all-gather | bytes 10752 | tf_op jit(solution)/shard_map/all_gather | solution.py:60
  151.6 0.1 reshape.84
  152.4 1.7 %fusion.9 = f32[1,192,1024]{2,1,0:T(8,128)} fusion(bf16[1152,1024]{1,0:T(8,128)(2,1)S(1)} %bitcast.44, f32[192,1152]{1,0:T(8,128)S(1)} %get-tuple-element.165, s32[192]{0:T(256)S(1)} %bitcast.47, f32[1152]{0:T(1024)S(1)} %log_add_fusion, f32[192]{0:T(256)S(1)} %get-tuple-element.160), kind=kOutput, calls=%fused_computation.11 | convolution fusion | flops 454729728 | bytes 4036608 | tf_op jit(solution)/shard_map/dot_general | solution.py:131
  154.1 0.0 all-gather.6.cloned.1.call-done
  154.1 4.9 %fusion.6 = f32[1,192,1024]{2,1,0:T(8,128)} fusion(bf16[1,1152,1024]{2,1,0:T(8,128)(2,1)} %all-gather.6.cloned.1.call-done, s32[1152]{0:T(1024)S(1)} %fusion.28, f32[192]{0:T(256)S(1)} %get-tuple-element.158, f32[1152]{0:T(1024)S(1)} %slice_reduce_fusion, s32[192]{0:T(256)S(1)} %iota_add_fusion, bf16[1,192,1024]{2,1,0:T(8,128)(2,1)} %param.6), kind=kOutput, calls=%fused_computation.9 | convolution fusion | flops 907935744 | bytes 3549696 | tf_op jit(solution)/shard_map/dot_general | solution.py:146
  (24 shorter events, 0.4 us)
Async XLA Ops:
  9.9 64.0 %all-to-all-start = ((bf16[6,1,192,1024]{3,2,1,0:T(8,128)(2,1)}), bf16[6,1,192,1024]{3,2,1,0:T(8,128)(2,1)S(1)}, u32[]{:S(2)}, u32[]{:S(2)}) async-start(bf16[6,1,192,1024]{3,2,1,0:T(8,128)(2,1)} %broadcast_in_dim.10), calls=%async_computation | async-start | bytes 4718592 | tf_op jit(solution)/shard_map/all_to_all | solution.py:23
  23.9 52.0 %copy-start = (s32[1,192]{1,0:T(1,128)S(1)}, s32[1,192]{1,0:T(1,128)}, u32[]{:S(2)}) copy-start(s32[1,192]{1,0:T(1,128)} %param.7) | copy-start | bytes 2308
  23.9 130.2 %all-gather.6.cloned.1.call-start = ((), (), s32[]{:S(2)}) async-start(), calls=%async_computation.1 | async-start | bytes 2752512 | tf_op jit(solution)/shard_map/all_gather | solution.py:137
Sparse Core Ops, SparseCore 0:
  27.1 54.5 all-gather.5
where the time goes:
time: 167 us
  blocking collectives  72 us (43%)
  waiting for transfers between devices  49.9 us (30%)
  between operations  17.2 us (10%)
  starting transfers between devices  14.1 us (8%)
  matrix products  8.66 us (5%)
  local copies, waits for them, and re-layouts  3.09 us (2%)
  other arithmetic  1.91 us (1%)
    psum x5, blocking collectives, by_axis(): x = lax.psum(x, axis)  52.6 us
    all_to_all x1, waiting for transfers between devices, sent_to_all(): return lax.all_to_all(copies, axis, split_axis=0, concat_axis=0, tiled=True)  49.2 us
    all_to_all x1, starting transfers between devices, sent_to_all(): return lax.all_to_all(copies, axis, split_axis=0, concat_axis=0, tiled=True)  14 us
    all_gather x1, blocking collectives, collected_together(): both, at, found = (lax.all_gather(jnp.concatenate(lines), axis), 0, {})  10.1 us
    all_gather x1, blocking collectives, gather_turned(): out, at, done = (lax.all_gather(both, axis, axis=0, tiled=True), 0, [])  9.31 us
    dot_general x1, matrix products, local(): summed = jnp.dot(weight_back, piece, preferred_element_type=jnp.float32)  4.92 us
  transfers between devices with their start and end apart: 2, of which 1 were waited for; matrix products, arithmetic and copies ran while one was open for 4% of the time, Pallas kernels for 0%

commit v1 on v0

v1 whole, which is shorter than its diff:
```python
import functools

import jax
import jax.numpy as jnp
from jax import lax
from jax.experimental import pallas as pl
from jax.experimental.pallas import tpu as pltpu
from jax.sharding import Mesh
from jax.sharding import PartitionSpec as P

GRP = ("grp_0", "grp_1")
BLK = ("blk_0", "blk_1", "blk_2")
MESH = pl.DeviceIdType.MESH
F32 = jnp.float32
BF16 = jnp.bfloat16

SCALE = 0.125
LANES = 128
R = 64
NC = 3
KS = 2
ZS = 3
ROWS = R * NC
BLOCK = R * KS
TOTAL = ROWS * KS * ZS
MIDW = NC * BLOCK
NT = TOTAL // LANES
REDUCE = ("blk_1", "blk_2", "blk_0")


def mid_base(n):
    return n * BLOCK


def end_base(z, n):
    return MIDW + n * 2 * BLOCK + (z // 2) * BLOCK


def row_ids(q):
    in_mid = q < MIDW
    e = q - MIDW
    n = jnp.where(in_mid, q >> 7, e >> 8)
    z = jnp.where(in_mid, 1, ((e >> 7) & 1) * 2)
    k = (q >> 6) & 1
    return (z * KS + k) * ROWS + n * R + (q & (R - 1))


def fold(x, op):
    parts = [x[8 * i : 8 * i + 8] for i in range(x.shape[0] // 8)]
    while len(parts) > 1:
        parts = [op(parts[i], parts[i + 1]) if i + 1 < len(parts) else parts[i] for i in range(0, len(parts), 2)]
    return parts[0]


def tree(parts, op):
    parts = list(parts)
    while len(parts) > 1:
        parts = [op(parts[i], parts[i + 1]) if i + 1 < len(parts) else parts[i] for i in range(0, len(parts), 2)]
    return parts[0]


def add(a, b):
    return a + b


def dot_nt(a, b):
    return lax.dot_general(a, b, (((1,), (1,)), ((), ())), preferred_element_type=F32)


def kernel(
    axes,
    text, image, prow, pcol,
    gt, gi, loss,
    t_own, tb, ib, pb, plan, gcol, s_own, sp, runm, runs, clcol, cl, rl, wb, gx, lbuf, lfin,
    loc, bsend, ri, rt, rp, rg, rs, rloss, rfin,
):
    z = lax.axis_index("grp_0")
    k = lax.axis_index("grp_1")
    other = 1 - k
    width = text.shape[1]
    ks = k * R

    sends = []

    def send(src, dst, rsem, **dev):
        copy = pltpu.make_async_remote_copy(
            src_ref=src,
            dst_ref=dst,
            send_sem=bsend.at[len(sends)],
            recv_sem=rsem,
            device_id=dev,
            device_id_type=MESH,
        )
        copy.start()
        sends.append(copy)

    def wait_for(dst, rsem):
        pltpu.make_async_remote_copy(
            src_ref=dst,
            dst_ref=dst,
            send_sem=bsend.at[0],
            recv_sem=rsem,
            device_id={"grp_1": other},
            device_id_type=MESH,
        ).wait_recv()

    def at_rows(ref, start):
        return ref.at[pl.ds(pl.multiple_of(start, R), R), :]

    def sem_of(sems, zz, n, kk):
        return sems.at[zz * (NC * KS) + n * KS + kk]

    def own_rows(ref, n):
        return ref.at[pl.ds(n * R, R), :]

    def load_own(base, with_text):
        copies = []

        def load(src, dst):
            copy = pltpu.make_async_copy(src, dst, loc.at[len(copies)])
            copy.start()
            copies.append(copy)

        for n in range(NC):
            load(own_rows(image, n), at_rows(ib, base(n) + ks))
        load(text, t_own)
        pb[z * KS + k] = prow[...]
        if with_text:
            for n in range(NC):
                load(own_rows(text, n), at_rows(tb, base(n) + ks))
        return copies

    def score_own(start, size):
        block = ib[pl.ds(start, size), :]
        s_own[:, pl.ds(start, size)] = dot_nt(t_own[...], block) * SCALE

    def text_gradient():
        tiles = [slice(t * LANES, (t + 1) * LANES) for t in range(NT)]
        for n in range(NC):
            rows = slice(n * R, (n + 1) * R)
            top = jnp.max(tree([s_own[rows, t] for t in tiles], jnp.maximum), axis=1, keepdims=True)
            total = jnp.sum(tree([jnp.exp(s_own[rows, t] - top) for t in tiles], add), axis=1, keepdims=True)
            row_lse = top + jnp.log(total)
            for t in tiles:
                s = s_own[rows, t]
                q = lax.broadcasted_iota(jnp.int32, (1, LANES), 1) + t.start
                hit = pcol[rows, :] == row_ids(q)
                w = jnp.exp(s - row_lse) + jnp.exp(s - cl[0:1, t]) - jnp.where(hit, 2.0, 0.0)
                wb[rows, t] = w.astype(BF16)
        for h in range(width // 256):
            cols = slice(h * 256, (h + 1) * 256)
            gt[:, cols] = jnp.dot(wb[...], ib[:, cols], preferred_element_type=F32) * (SCALE * 0.5)

    def finish():
        for copy in sends:
            copy.wait_send()
        sends.clear()

    barrier = pltpu.get_barrier_semaphore()

    def ends():
        far = 2 - z
        base = functools.partial(end_base, z)
        copies = load_own(base, False)
        pl.semaphore_signal(barrier, inc=1, device_id={"grp_1": other}, device_id_type=MESH)
        pl.semaphore_signal(barrier, inc=1, device_id={"grp_0": 1}, device_id_type=MESH)
        for copy in copies:
            copy.wait()
        pl.semaphore_wait(barrier, 2)

        def mine(n):
            return at_rows(ib, base(n) + ks)

        send(pb.at[z * KS + k], pb.at[z * KS + k], rp.at[z * KS + k], grp_0=1)
        for n in range(NC):
            send(mine(n), mine(n), sem_of(ri, z, n, k), grp_0=1)
        for n in range(NC):
            send(mine(n), mine(n), sem_of(ri, z, n, k), grp_1=other)
        for n in range(NC):
            send(own_rows(t_own, n), at_rows(tb, base(n) + ks), sem_of(rt, z, n, k), grp_0=1)

        for n in range(NC):
            part = at_rows(ib, mid_base(n) + ks)
            wait_for(part, sem_of(ri, 1, n, k))
            send(part, part, sem_of(ri, 1, n, k), grp_1=other)
        for n in range(NC):
            wait_for(at_rows(ib, base(n) + other * R), sem_of(ri, z, n, other))
            wait_for(at_rows(ib, mid_base(n) + other * R), sem_of(ri, 1, n, other))
        score_own(0, MIDW)
        for n in range(NC):
            part = at_rows(ib, end_base(far, n) + ks)
            wait_for(part, sem_of(ri, far, n, k))
            send(part, part, sem_of(ri, far, n, k), grp_1=other)
            wait_for(at_rows(ib, end_base(far, n) + other * R), sem_of(ri, far, n, other))
            score_own(MIDW + n * 2 * BLOCK, 2 * BLOCK)
        wait_for(cl, rs.at[0])
        text_gradient()
        for n in range(NC):
            part = gx.at[n, pl.ds(0, R), :]
            wait_for(part, rg.at[n])
            gi[n * R : (n + 1) * R, :] = gx[n, 0:R, :].astype(F32)
        wait_for(lfin, rfin.at[0])
        loss[...] = lfin[...]
        finish()

    def middle():
        copies = load_own(mid_base, True)
        pl.semaphore_signal(barrier, inc=1, device_id={"grp_1": other}, device_id_type=MESH)
        pl.semaphore_signal(barrier, inc=1, device_id={"grp_0": 0}, device_id_type=MESH)
        pl.semaphore_signal(barrier, inc=1, device_id={"grp_0": 2}, device_id_type=MESH)
        greeted = 3
        for name, size in axes:
            for step in range(1, size):
                peer = lax.rem(lax.axis_index(name) + step, size)
                pl.semaphore_signal(barrier, inc=1, device_id={name: peer}, device_id_type=MESH)
                greeted += 1
        for copy in copies:
            copy.wait()
        pl.semaphore_wait(barrier, greeted)

        def mine(ref, n):
            return at_rows(ref, mid_base(n) + ks)

        for n in range(NC):
            for e in (0, 2):
                send(mine(ib, n), mine(ib, n), sem_of(ri, 1, n, k), grp_0=e)
        send(pb.at[KS + k], pb.at[KS + k], rp.at[KS + k], grp_1=other)
        for n in range(NC):
            send(mine(ib, n), mine(ib, n), sem_of(ri, 1, n, k), grp_1=other)
        for n in range(NC):
            send(mine(tb, n), mine(tb, n), sem_of(rt, 1, n, k), grp_1=other)

        def ids(i, _):
            rows = pl.ds(pl.multiple_of(i * LANES, LANES), LANES)
            q = lax.broadcasted_iota(jnp.int32, (LANES, LANES), 0) + i * LANES
            gcol[rows, :] = row_ids(q)
            runm[rows, :] = jnp.full((LANES, LANES), -1e30, F32)
            runs[rows, :] = jnp.zeros((LANES, LANES), F32)
            return 0

        lax.fori_loop(0, NT, ids, 0)

        for e in (0, 2):
            slot = e * KS + k
            wait_for(pb.at[slot], rp.at[slot])
            send(pb.at[slot], pb.at[slot], rp.at[slot], grp_1=other)
        for n in range(NC):
            for e in (0, 2):
                part = at_rows(ib, end_base(e, n) + ks)
                wait_for(part, sem_of(ri, e, n, k))
                send(part, part, sem_of(ri, e, n, k), grp_0=2 - e)
                send(part, part, sem_of(ri, e, n, k), grp_1=other)
        for zz in range(ZS):
            wait_for(pb.at[zz * KS + other], rp.at[zz * KS + other])
            for n in range(NC):
                start = mid_base(n) if zz == 1 else end_base(zz, n)
                plan[0:1, start : start + BLOCK] = pb[zz * KS, n : n + 1, :] + pb[zz * KS + 1, n : n + 1, :]
        for n in range(NC):
            wait_for(at_rows(tb, mid_base(n) + other * R), sem_of(rt, 1, n, other))
            wait_for(at_rows(ib, mid_base(n) + other * R), sem_of(ri, 1, n, other))
            for e in (0, 2):
                wait_for(at_rows(ib, end_base(e, n) + other * R), sem_of(ri, e, n, other))
        score_own(0, TOTAL)

        def scores_and_stats(start, size, hits):
            sp[:, start : start + size] = dot_nt(ib[...], tb[start : start + size, :]) * SCALE
            tiles = [slice(start + t * LANES, start + (t + 1) * LANES) for t in range(size // LANES)]

            def first(i, carry):
                tops, hits = carry
                rows = pl.ds(pl.multiple_of(i * LANES, LANES), LANES)
                vs = [sp[rows, t] for t in tiles]
                old = runm[rows, :]
                top = jnp.maximum(jnp.max(tree(vs, jnp.maximum), axis=1, keepdims=True), old)
                fresh = jnp.sum(tree([jnp.exp(v - top) for v in vs], add), axis=1, keepdims=True)
                runs[rows, :] = runs[rows, :] * jnp.exp(old - top) + fresh
                runm[rows, :] = top
                ids = gcol[rows, :]
                found = [jnp.where(ids == plan[0:1, t], v, 0.0) for t, v in zip(tiles, vs)]
                hits = hits + fold(tree(found, add), add)
                return tuple(jnp.maximum(m, fold(v, jnp.maximum)) for m, v in zip(tops, vs)), hits

            none = jnp.full((8, LANES), -1e30, F32)
            tops, hits = lax.fori_loop(0, NT, first, (tuple(none for _ in tiles), hits))
            tops = [jnp.max(m, axis=0, keepdims=True) for m in tops]

            def second(i, sums):
                rows = pl.ds(pl.multiple_of(i * LANES, LANES), LANES)
                return tuple(s + fold(jnp.exp(sp[rows, t] - m), add) for s, t, m in zip(sums, tiles, tops))

            sums = lax.fori_loop(0, NT, second, tuple(jnp.zeros((8, LANES), F32) for _ in tiles))
            for t, m, s in zip(tiles, tops, sums):
                rl[0:1, t] = m + jnp.log(jnp.sum(s, axis=0, keepdims=True))
            return hits

        hits = scores_and_stats(0, MIDW, jnp.zeros((8, LANES), F32))
        for n in range(NC):
            for e in (0, 2):
                part = at_rows(tb, end_base(e, n) + ks)
                wait_for(part, sem_of(rt, e, n, k))
                send(part, part, sem_of(rt, e, n, k), grp_1=other)
            for e in (0, 2):
                wait_for(at_rows(tb, end_base(e, n) + other * R), sem_of(rt, e, n, other))
            hits = scores_and_stats(MIDW + n * 2 * BLOCK, 2 * BLOCK, hits)

        eye = lax.broadcasted_iota(jnp.int32, (LANES, LANES), 0) == lax.broadcasted_iota(jnp.int32, (LANES, LANES), 1)
        lse_sum = jnp.zeros((1, LANES), F32)
        for i in range(NT):
            rows = slice(i * LANES, (i + 1) * LANES)
            lse = runm[rows, :] + jnp.log(runs[rows, :])
            clcol[rows, :] = lse
            line = jnp.sum(fold(jnp.where(eye, lse, 0.0), add), axis=0, keepdims=True)
            cl[0:1, rows] = line
            lse_sum = lse_sum + line + rl[0:1, rows]
        part = jnp.sum(lse_sum, axis=1, keepdims=True) - 2.0 * jnp.sum(
            jnp.sum(hits, axis=0, keepdims=True), axis=1, keepdims=True
        )

        def weights(start, row):
            rows = pl.ds(pl.multiple_of(start, R), R)
            col = clcol[rows, :]
            ids = gcol[rows, :]
            for t in range(NT):
                lanes = slice(t * LANES, (t + 1) * LANES)
                s = sp[rows, lanes]
                hit = ids == plan[0:1, lanes]
                w = jnp.exp(s - col) + jnp.exp(s - rl[0:1, lanes]) - jnp.where(hit, 2.0, 0.0)
                wb[row : row + R, lanes] = w.astype(BF16)

        def exchange(name, size, off, value):
            me = lax.axis_index(name)
            lbuf[off + me] = jnp.broadcast_to(value, (8, LANES))
            for step in range(1, size):
                peer = lax.rem(me + step, size)
                send(lbuf.at[off + me], lbuf.at[off + me], rloss.at[off + me], **{name: peer})

        def collected(name, size, off):
            me = lax.axis_index(name)
            for step in range(1, size):
                peer = lax.rem(me + step, size)
                wait_for(lbuf.at[off + peer], rloss.at[off + peer])
            total = lbuf[off]
            for i in range(1, size):
                total = total + lbuf[off + i]
            return total[0:1, :]

        offs = [sum(size for _, size in axes[:i]) for i in range(len(axes))]
        exchange(*axes[0], offs[0], part)
        for e in (0, 2):
            send(cl, cl, rs.at[0], grp_0=e)

        for n in range(NC):
            weights(end_base(0, n) + ks, 0)
            weights(end_base(2, n) + ks, R)
            for h in range(width // 256):
                cols = slice(h * 256, (h + 1) * 256)
                g = jnp.dot(wb[0 : 2 * R, :], tb[:, cols], preferred_element_type=F32) * (SCALE * 0.5)
                gx[n, :, cols] = g.astype(BF16)
            for e in (0, 2):
                send(gx.at[n, pl.ds((e // 2) * R, R), :], gx.at[n, pl.ds(0, R), :], rg.at[n], grp_0=e)

        value = collected(*axes[0], offs[0])
        exchange(*axes[1], offs[1], value)
        for n in range(NC):
            weights(mid_base(n) + ks, n * R)
        for h in range(width // 256):
            cols = slice(h * 256, (h + 1) * 256)
            gi[:, cols] = jnp.dot(wb[...], tb[:, cols], preferred_element_type=F32) * (SCALE * 0.5)
        value = collected(*axes[1], offs[1])
        exchange(*axes[2], offs[2], value)
        text_gradient()
        value = collected(*axes[2], offs[2])
        groups = 1
        for _, size in axes:
            groups *= size
        lfin[...] = jnp.broadcast_to(value * (1.0 / (2.0 * TOTAL * groups)), (8, LANES))
        for e in (0, 2):
            send(lfin, lfin, rfin.at[0], grp_0=e)
        loss[...] = lfin[...]
        finish()

    pl.when(z != 1)(ends)
    pl.when(z == 1)(middle)


def local(axes, text, image, pair_index):
    rows, width = text.shape[1:]
    assert rows == ROWS
    pairs = pair_index[0]
    k = lax.axis_index("grp_1")
    pieces = pairs.reshape(NC, R)
    none = jnp.zeros_like(pieces)
    line = jnp.where(
        k == 0, jnp.concatenate([pieces, none], 1), jnp.concatenate([none, pieces], 1)
    )
    line = jnp.pad(line, ((0, 8 - NC), (0, 0)))
    column = jnp.broadcast_to(pairs[:, None], (rows, LANES))
    slots = sum(size for _, size in axes)
    vmem = pl.BlockSpec(memory_space=pltpu.VMEM)
    hbm = pl.BlockSpec(memory_space=pltpu.HBM)
    dma = pltpu.SemaphoreType.DMA
    gt, gi, loss = pl.pallas_call(
        functools.partial(kernel, axes),
        out_shape=(
            jax.ShapeDtypeStruct((rows, width), F32),
            jax.ShapeDtypeStruct((rows, width), F32),
            jax.ShapeDtypeStruct((8, LANES), F32),
        ),
        in_specs=[hbm, hbm, vmem, vmem],
        out_specs=[vmem, vmem, vmem],
        scratch_shapes=[
            pltpu.VMEM((rows, width), BF16),
            pltpu.VMEM((TOTAL, width), BF16),
            pltpu.VMEM((TOTAL, width), BF16),
            pltpu.VMEM((ZS * KS, 8, LANES), jnp.int32),
            pltpu.VMEM((1, TOTAL), jnp.int32),
            pltpu.VMEM((TOTAL, LANES), jnp.int32),
            pltpu.VMEM((rows, TOTAL), F32),
            pltpu.VMEM((TOTAL, TOTAL), F32),
            pltpu.VMEM((TOTAL, LANES), F32),
            pltpu.VMEM((TOTAL, LANES), F32),
            pltpu.VMEM((TOTAL, LANES), F32),
            pltpu.VMEM((1, TOTAL), F32),
            pltpu.VMEM((1, TOTAL), F32),
            pltpu.VMEM((rows, TOTAL), BF16),
            pltpu.VMEM((NC, 2 * R, width), BF16),
            pltpu.VMEM((slots, 8, LANES), F32),
            pltpu.VMEM((8, LANES), F32),
            dma((2 * NC + 2,)),
            dma((72,)),
            dma((ZS * NC * KS,)),
            dma((ZS * NC * KS,)),
            dma((ZS * KS,)),
            dma((NC,)),
            dma((1,)),
            dma((slots,)),
            dma((1,)),
        ],
        compiler_params=pltpu.CompilerParams(
            collective_id=0, has_side_effects=True, vmem_limit_bytes=48 * 1024 * 1024
        ),
    )(
        pltpu.with_memory_space_constraint(text[0], pltpu.HBM),
        pltpu.with_memory_space_constraint(image[0], pltpu.HBM),
        line,
        column,
    )
    return gt[None], gi[None], loss[0, 0]


def solution(mesh):
    torus = Mesh(mesh.devices.reshape(8, 4, 4, 3, 2), (*BLK, *GRP))
    axes = tuple((name, torus.shape[name]) for name in REDUCE)
    in_specs = (P(BLK, GRP, None), P(BLK, GRP, None), P(BLK, GRP))
    out_specs = (P(BLK, GRP, None), P(BLK, GRP, None), P())
    return jax.shard_map(
        functools.partial(local, axes), mesh=torus, in_specs=in_specs, out_specs=out_specs, check_vma=False
    )
```

time: 167 us -> 69.3 us (0.41)
  the two profiles are of different devices: /device:TPU:1 before, /device:TPU:2 now
where the time goes in v1:
time: 69.3 us; the launch traced here: 69.1 us
  Pallas kernels  64.6 us (93%)
  local copies, waits for them, and re-layouts  3.11 us (4%)
  other arithmetic  0.74 us (1%)
    pallas_call x1, Pallas kernels, local(): pl.pallas_call(functools.partial(kernel, axes), out_shape=(jax.ShapeDtype...  64.6 us
    unnamed x5, local copies, waits for them, and re-layouts  2.43 us

profile of v1, /device:TPU:2, one launch (start us, length us, event | category | flops | bytes accessed | tf_op | source)
XLA Modules:
  0.0 69.1 jit_solution(7975661350068102727)
XLA Ops:
  0.6 0.0 copy-start
  0.6 0.5 broadcast.9
  1.2 0.2 copy-done
  1.3 0.7 reduce.3
  2.0 0.1 reshape_squeeze.3
  2.1 0.1 pad_select_fusion
  2.2 0.1 broadcast_in_dim.15.pcol
  2.2 64.6 %shard_map.58 = (f32[192,1024]{1,0:T(8,128)S(1)}, f32[192,1024]{1,0:T(8,128)S(1)}, f32[8,128]{1,0:T(8,128)S(1)}) custom-call(bf16[192,1024]{1,0:T(8,128)(2,1)} %bitcast.8, bf16[192,1024]{1,0:T(8,128)(2,1)} %bitcast.9, s32[8,128]{1,0:T(8,128)S(1)} %pad.6.prow, s32[192,128]{1,0:T(8,128)S(1)} %broadcast_in_dim.15.pcol), custom_call_target="tpu_custom_call" | custom-call | tf_op jit(solution)/shard_map/pallas_call | solution.py:402
  66.8 0.5 slice.3
  67.3 0.9 %copy.8 = f32[1,192,1024]{2,1,0:T(8,128)} copy(f32[1,192,1024]{2,1,0:T(8,128)S(1)} %bitcast.7) | data formatting | bytes 1572864
  68.2 0.9 %copy.9 = f32[1,192,1024]{2,1,0:T(8,128)} copy(f32[1,192,1024]{2,1,0:T(8,128)S(1)} %bitcast.6) | data formatting | bytes 1572864
  (1 shorter events, 0.0 us)
Async XLA Ops:
  0.6 0.7 copy-start
